TPU v7x, 32 devices: a whole 2x2x4 slice. The times are simulated.
32 devices in a mesh: samples: 8 (over z, y), groups: 4 (over x, core).
Axes of the slice: x: 2, y: 2, z: 4, core: 2. Of those that a mesh axis runs over, the one named last changes fastest.
Arguments:
- observed: bfloat16 [128, 10240], P('samples', 'groups'), may hold values from -200 to 200
- labels: int32 [10240], P('groups'), may hold values from 0 to 31, as said below
- comp_sizes: int32 [32], P('groups'), may hold values from 128 to 512, as said below
Outputs:
- whitened: bfloat16 [128, 10240], P('samples', 'groups')
Inputs may be any that keep to these rules, and one draw needn't show every extreme that they name: Group g's columns (g * 2560 to (g + 1) * 2560 - 1) carry exactly the labels g * 8 to (g + 1) * 8 - 1, and label c stands on exactly comp_sizes[c] columns. `comp_sizes`: in every group one component has exactly 512 variables; components 2k and 2k + 1 (k = 0, 1, ...) together have exactly 640 variables.
All inputs are finite; a program needn't handle non-finite values. Where the computation divides by a largest or mean magnitude, that divisor is 1e-20 or more.
Results may differ from a plain program's by a relative error of at most 0.0038.
The roundings to bfloat16 on the way count: a program that leaves them out, or rounds other values in their place, can miss the bound.
Values may be sent and summed in bfloat16 or wider, within the bound.
A program may use at most 64 MiB of HBM per device.

v0:
```python
import functools

import jax
import jax.numpy as jnp
from jax import lax
from jax.experimental import pallas as pl
from jax.experimental.pallas import tpu as pltpu
from jax.sharding import PartitionSpec as P

CMAX = 512
ITERS = 5
LANES = 128
UNROLL_LIMIT = 1024

shrink = 0.2
ridge = 0.5

BF16 = jnp.bfloat16
F32 = jnp.float32
HIGHEST = lax.Precision.HIGHEST
MESH = pl.DeviceIdType.MESH
VMEM = pl.BlockSpec(memory_space=pltpu.VMEM)


def loop(count, step, carry, unrolled):
    if unrolled:
        for i in range(count):
            carry = step(i, carry)
        return carry
    return lax.fori_loop(0, count, step, carry)


def lane_gather(values, index):
    return jnp.take_along_axis(values, index, axis=1)


def thirds(value):
    high = value.astype(BF16)
    rest = value - high.astype(F32)
    middle = rest.astype(BF16)
    low = (rest - middle.astype(F32)).astype(BF16)
    return high, middle, low


def products(lefts, right):
    extent = right.shape[0]
    high, middle, low = thirds(right)
    left_high, left_middle, left_low = thirds(jnp.concatenate(lefts, axis=0))
    pair = jnp.concatenate([high, middle], axis=1)
    main = jnp.dot(
        jnp.concatenate([left_high, left_middle], axis=1),
        jnp.concatenate([pair, pair], axis=0),
        preferred_element_type=F32,
    )
    small = jnp.dot(
        jnp.concatenate([left_high, left_low], axis=1),
        jnp.concatenate([low, high], axis=0),
        preferred_element_type=F32,
    )
    whole = (small + main[:, extent:]) + main[:, :extent]
    return [whole[i * extent : (i + 1) * extent] for i in range(len(lefts))]


def eye(extent, value):
    down = lax.broadcasted_iota(jnp.int32, (extent, extent), 0)
    across = lax.broadcasted_iota(jnp.int32, (extent, extent), 1)
    return jnp.where(down == across, jnp.broadcast_to(value, (extent, extent)), 0.0)


def scale_and_bound(samples, gram_peak, squares, size, average):
    target = squares / samples / size
    lift = shrink * target + ridge * average
    weight = (1.0 - shrink) / samples
    return weight, lift, weight * gram_peak + lift


def whiten_rows(block, turned, inner, squares, peak, size, average, out):
    samples = block.shape[0]
    weight, lift, bound = scale_and_bound(samples, peak, squares, size, average)
    inverse_bound = 1.0 / bound
    v = inner * (weight * inverse_bound)
    e = 1.0 - lift * inverse_bound
    c = jnp.ones_like(e)
    u = d = None
    for step in range(ITERS):
        lefts = [] if step == ITERS - 1 else [v] if step == 0 else [v, u]
        results = products(lefts + ([d] if step > 1 else []), v)
        if step == 0:
            d, u = eye(samples, -c), eye(samples, 2.0 * e) - v
        else:
            through = results[-1] if step > 1 else -v
            d = (1.0 + e) * d - c * u - through
            if lefts:
                u = 2.0 * e * u - results[1]
        if lefts:
            v = 2.0 * e * v - results[0]
        c = c * (1.0 + e)
        e = e * e
    mixed = sum(jnp.dot(piece, block, preferred_element_type=F32) for piece in reversed(thirds(d)))
    mixed = mixed * (weight * inverse_bound)
    width = block.shape[1]
    stacked = jnp.concatenate(thirds(mixed), axis=0)
    wide_turned = jnp.concatenate([turned] * 3, axis=1)
    inverse = jnp.dot(wide_turned, stacked, preferred_element_type=F32) * inverse_bound
    inverse = (inverse + eye(width, c * inverse_bound)).astype(BF16)
    out(jnp.dot(block, inverse, preferred_element_type=F32).astype(BF16))


def whiten_columns(block, gram_ref, current_ref, squares, peak, size, average, out):
    samples, width = block.shape
    weight, lift, bound = scale_and_bound(samples, peak, squares, size, average)
    gram_ref[...] = weight * gram_ref[...] + eye(width, lift)
    current_ref[...] = eye(width, 1.0 / bound)

    def sweep(i, carry):
        current = current_ref[...]
        product = jnp.dot(gram_ref[...], current, precision=HIGHEST, preferred_element_type=F32)
        current_ref[...] = jnp.dot(
            current, eye(width, jnp.full((1, 1), 2.0, F32)) - product, precision=HIGHEST, preferred_element_type=F32
        )
        return carry

    lax.fori_loop(0, ITERS, sweep, 0)
    out(jnp.dot(block, current_ref[...].astype(BF16), preferred_element_type=F32).astype(BF16))


def fused_kernel(
    samples_count,
    groups_count,
    entries,
    size_hbm,
    label_hbm,
    observed_hbm,
    result_ref,
    size_ref,
    label_ref,
    observed_ref,
    load_sem,
    sorted_ref,
    high_ref,
    turn_ref,
    place_ref,
    filled_ref,
    packed_ref,
    held_ref,
    done_ref,
    back_ref,
    energy_ref,
    group_ref,
    total_ref,
    all_ref,
    *rest,
):
    *work, group_send, group_recv, total_send, total_recv, out_send, out_recv, back_send, back_recv = rest
    me = lax.axis_index("samples")
    group = lax.axis_index("groups")
    _, slot_here, rows, width = packed_ref.shape
    samples = samples_count * rows
    slots = samples_count * slot_here
    tiles = sorted_ref.shape[0]
    parts = width // LANES
    unrolled = tiles * slots <= UNROLL_LIMIT
    order = sorted(range(1, samples_count), key=lambda k: abs(2 * k - samples_count))

    def ahead(k):
        return lax.rem(me + k, samples_count)

    def behind(k):
        return lax.rem(me + samples_count - k, samples_count)

    def copy(source, target, send, recv, sample, other):
        return pltpu.make_async_remote_copy(
            src_ref=source,
            dst_ref=target,
            send_sem=send,
            recv_sem=recv,
            device_id=(sample, other),
            device_id_type=MESH,
        )

    def columns(t):
        return pl.ds(t * LANES if isinstance(t, int) else pl.multiple_of(t * LANES, LANES), LANES)

    loads = [
        pltpu.make_async_copy(source, target, load_sem.at[i])
        for i, (source, target) in enumerate(
            ((label_hbm, label_ref), (observed_hbm, observed_ref), (size_hbm, size_ref))
        )
    ]
    for item in loads:
        item.start()
    barrier = pltpu.get_barrier_semaphore()
    for k in range(1, samples_count):
        pl.semaphore_signal(barrier, inc=1, device_id=(ahead(k), group), device_id_type=MESH)
    for k in range(1, groups_count):
        other = lax.rem(group + k, groups_count)
        pl.semaphore_signal(barrier, inc=1, device_id=(me, other), device_id_type=MESH)

    for item in loads:
        item.wait()

    first = group * slots
    slot = lax.broadcasted_iota(jnp.int32, (slots, LANES), 0)
    down = lax.broadcasted_iota(jnp.int32, (LANES, LANES), 0)
    across = lax.broadcasted_iota(jnp.int32, (LANES, LANES), 1)
    upto = (down <= across).astype(BF16)
    ones = jnp.ones((LANES, LANES), BF16)

    def compare(t):
        label = label_ref[pl.ds(t, 1), :] - first
        return (label == slot).astype(F32), (label < slot).astype(F32)

    def counts(equal, less):
        rank = jnp.dot(equal.astype(BF16), upto, preferred_element_type=F32) - 1.0
        count = jnp.dot(equal.astype(BF16), ones, preferred_element_type=F32)
        before = jnp.dot(less.astype(BF16), ones, preferred_element_type=F32)
        return rank, count, before

    if unrolled:
        pairs = [compare(t) for t in range(tiles)]
        stacked = counts(*(jnp.concatenate(items, axis=0) for items in zip(*pairs)))

    def sort_tile(t, carry):
        base, energy = carry
        if unrolled:
            equal = pairs[t][0]
            rank, count, before = (item[t * slots : (t + 1) * slots] for item in stacked)
        else:
            equal, less = compare(t)
            rank, count, before = counts(equal, less)
        local = jnp.sum(equal * (before + rank), axis=0, keepdims=True).astype(jnp.int32)
        whole = slot.astype(F32) * CMAX + base + rank
        place_ref[pl.ds(t, 1), :] = jnp.sum(equal * whole, axis=0, keepdims=True).astype(jnp.int32)
        block = observed_ref[:, columns(t)]
        choose = (down == local).astype(BF16)
        sorted_ref[t] = lax.dot_general(
            block, choose, (((1,), (1,)), ((), ())), preferred_element_type=F32
        )
        high_ref[t] = (base + count).astype(jnp.int32)
        turn_ref[t] = (before - base).astype(jnp.int32)
        wide = block.astype(F32)
        square = wide * wide
        for r in range(0, rows, 8):
            energy = energy + square[r : r + 8]
        return base + count, energy

    start = (jnp.zeros((slots, LANES), F32), jnp.zeros((8, LANES), F32))
    _, total = loop(tiles, sort_tile, start, unrolled)
    energy_ref[...] = total

    lane = lax.broadcasted_iota(jnp.int32, (rows, LANES), 1)

    def pack_slot(sample, h, target):
        c = sample * slot_here + h

        def add_tile(i, packed):
            t = tiles - 1 - i
            high = jnp.broadcast_to(high_ref[t, pl.ds(c, 1), :], (rows, LANES))
            turn = jnp.broadcast_to(turn_ref[t, pl.ds(c, 1), :], (rows, LANES))
            moved = lane_gather(sorted_ref[t], (lane + turn) & (LANES - 1))
            return tuple(
                jnp.where(lane + q * LANES < high, moved, packed[q])
                for q in range(parts)
            )

        zero = jnp.zeros((rows, LANES), F32)
        packed = loop(tiles, add_tile, (zero,) * parts, unrolled)
        for q in range(parts):
            target[:, q * LANES : (q + 1) * LANES] = packed[q].astype(BF16)

    group_copies = [
        copy(
            energy_ref,
            group_ref.at[k - 1],
            group_send.at[k - 1],
            group_recv.at[k - 1],
            me,
            lax.rem(group + k, groups_count),
        )
        for k in range(1, groups_count)
    ]
    out_copies = {
        k: copy(packed_ref.at[k], held_ref.at[k], out_send.at[k - 1], out_recv.at[k - 1], ahead(k), group)
        for k in order
    }
    total_copies = [
        copy(total_ref, all_ref.at[k - 1], total_send.at[k - 1], total_recv.at[k - 1], ahead(k), group)
        for k in order
    ]
    back_copies = [
        copy(done_ref.at[k], back_ref.at[me], back_send.at[k - 1], back_recv.at[me], behind(k), group)
        for k in order
    ]

    for k in order:
        for h in range(slot_here):
            pack_slot(ahead(k), h, packed_ref.at[k, h])
    pl.semaphore_wait(barrier, samples_count + groups_count - 2)
    for item in group_copies:
        item.start()
    for k in order:
        out_copies[k].start()
    for h in range(slot_here):
        pack_slot(me, h, held_ref.at[0, h])
    for item in group_copies:
        item.wait_recv()
    for k in range(groups_count - 1):
        total = total + group_ref[k]
    total_ref[...] = total
    for item in total_copies:
        item.start()
    for k in order:
        out_copies[k].wait_recv()

    average = None
    for h in range(slot_here):
        block = held_ref[:, h].reshape(samples, width)
        turned = block.T
        wide = block.astype(F32)
        squares = jnp.sum(jnp.sum(wide * wide, axis=0, keepdims=True), axis=1, keepdims=True)
        sums = jnp.zeros((1, width), F32)
        for r in range(0, width, LANES):
            part = jnp.dot(turned[r : r + LANES], block, preferred_element_type=F32)
            if work:
                work[0][r : r + LANES, :] = part
            sums = sums + jnp.sum(jnp.abs(part), axis=0, keepdims=True)
        peak = jnp.max(sums, axis=1, keepdims=True)
        if not work:
            inner = lax.dot_general(block, block, (((1,), (1,)), ((), ())), preferred_element_type=F32)
        if average is None:
            for item in total_copies:
                item.wait_recv()
            for k in range(samples_count - 1):
                total = total + all_ref[k]
            energy = jnp.sum(jnp.sum(total, axis=0, keepdims=True), axis=1, keepdims=True)
            average = energy / entries
        size = jnp.full((1, 1), size_ref[me * slot_here + h], jnp.int32).astype(F32)

        def out(value):
            done_ref[:, h] = value.reshape(samples_count, rows, width)

        if work:
            whiten_columns(block, work[0], work[1], squares, peak, size, average, out)
        else:
            whiten_rows(block, turned, inner, squares, peak, size, average, out)

    for item in back_copies:
        item.start()

    def fill(sample, source, opening):
        for h in range(slot_here):
            wide = [source[h, :, q * LANES : (q + 1) * LANES].astype(F32) for q in range(parts)]

            def fill_tile(t, carry):
                place = jnp.broadcast_to(place_ref[pl.ds(t, 1), :], (rows, LANES))
                index = place & (LANES - 1)
                tile = (place >> (LANES.bit_length() - 1)) - (sample * slot_here + h) * parts
                if opening and h == 0:
                    value = jnp.zeros((rows, LANES), F32)
                else:
                    value = filled_ref[t]
                for q in range(parts):
                    value = jnp.where(tile == q, lane_gather(wide[q], index), value)
                filled_ref[t] = value
                return carry

            loop(tiles, fill_tile, 0, unrolled)

    fill(me, done_ref.at[0], True)
    for k in reversed(order):
        copy(
            done_ref.at[k], back_ref.at[ahead(k)], back_send.at[k - 1], back_recv.at[ahead(k)], ahead(k), group
        ).wait_recv()
        fill(ahead(k), back_ref.at[ahead(k)], False)

    def finish(t, carry):
        result_ref[:, columns(t)] = filled_ref[t].astype(BF16)
        return carry

    loop(tiles, finish, 0, unrolled)
    for item in group_copies + list(out_copies.values()) + total_copies + back_copies:
        item.wait_send()


def body(observed, labels, comp_sizes):
    rows, width = observed.shape
    slots = comp_sizes.shape[0]
    samples_count = lax.axis_size("samples")
    groups_count = lax.axis_size("groups")
    slot_here = slots // samples_count
    tiles = width // LANES
    samples = rows * samples_count
    kind = pltpu.SemaphoreType.DMA
    table = pltpu.VMEM((tiles, slots, LANES), jnp.int32)
    wide_tiles = pltpu.VMEM((tiles, rows, LANES), F32)
    blocks = pltpu.VMEM((samples_count, slot_here, rows, CMAX), BF16)
    work = [pltpu.VMEM((CMAX, CMAX), F32)] * 2 if samples >= CMAX else []
    return pl.pallas_call(
        functools.partial(
            fused_kernel, samples_count, groups_count, float(samples * width * groups_count)
        ),
        out_shape=jax.ShapeDtypeStruct((rows, width), BF16),
        in_specs=[pl.BlockSpec(memory_space=pltpu.HBM)] * 3,
        out_specs=VMEM,
        scratch_shapes=[
            pltpu.SMEM(comp_sizes.shape, jnp.int32),
            pltpu.VMEM((tiles, LANES), jnp.int32),
            pltpu.VMEM((rows, width), BF16),
            kind((3,)),
            wide_tiles,
            table,
            table,
            pltpu.VMEM((tiles, LANES), jnp.int32),
            wide_tiles,
            blocks,
            blocks,
            blocks,
            blocks,
            pltpu.VMEM((8, LANES), F32),
            pltpu.VMEM((groups_count - 1, 8, LANES), F32),
            pltpu.VMEM((8, LANES), F32),
            pltpu.VMEM((samples_count - 1, 8, LANES), F32),
            *work,
            kind((groups_count - 1,)),
            kind((groups_count - 1,)),
            kind((samples_count - 1,)),
            kind((samples_count - 1,)),
            kind((samples_count - 1,)),
            kind((samples_count - 1,)),
            kind((samples_count - 1,)),
            kind((samples_count,)),
        ],
        compiler_params=pltpu.CompilerParams(
            collective_id=0, has_side_effects=True, vmem_limit_bytes=56 * 2**20
        ),
        name="whiten",
    )(comp_sizes, labels.reshape(tiles, LANES), observed)


def solution(mesh):
    return jax.shard_map(
        body,
        mesh=mesh,
        in_specs=(P("samples", "groups"), P("groups"), P("groups")),
        out_specs=P("samples", "groups"),
        check_vma=False,
    )
```

profile of v0, /device:TPU:0, one launch (start us, length us, event | category | flops | bytes accessed | tf_op | source)
XLA Modules:
  0.0 24.4 jit_solution(1486396146723544160)
XLA Ops:
  0.0 22.8 %whiten.1 = bf16[16,2560]{1,0:T(8,128)(2,1)} custom-call(s32[8]{0:T(128)} %size_hbm.1, s32[20,128]{1,0:T(8,128)} %bitcast.1, bf16[16,2560]{1,0:T(8,128)(2,1)} %observed_hbm.1), custom_call_target="tpu_custom_call" | custom-call | tf_op jit(solution)/shard_map/whiten/pallas_call | solution.py:398
  22.8 1.5 %copy.5 = bf16[16,2560]{1,0:T(8,128)(2,1)} copy(bf16[16,2560]{1,0:T(8,128)(2,1)} %whiten.1) | data formatting | bytes 163840
where the time goes:
time: 24.6 us; the launch traced here: 24.4 us
  Pallas kernels  22.8 us (93%)
  local copies, waits for them, and re-layouts  1.53 us (6%)
    pallas_call x1, Pallas kernels, body(): pl.pallas_call(functools.partial(fused_kernel, samples_count, groups_coun...  22.8 us
    unnamed x1, local copies, waits for them, and re-layouts  1.53 us

commit v1 on v0

--- a/solution.py
+++ b/solution.py
@@ -374,7 +374,7 @@
         fill(ahead(k), back_ref.at[ahead(k)], False)
 
     def finish(t, carry):
-        result_ref[:, columns(t)] = filled_ref[t].astype(BF16)
+        result_ref[:, columns(t)] = filled_ref[t]
         return carry
 
     loop(tiles, finish, 0, unrolled)
@@ -399,7 +399,7 @@
         functools.partial(
             fused_kernel, samples_count, groups_count, float(samples * width * groups_count)
         ),
-        out_shape=jax.ShapeDtypeStruct((rows, width), BF16),
+        out_shape=pltpu.VMEM((rows, width), F32),
         in_specs=[pl.BlockSpec(memory_space=pltpu.HBM)] * 3,
         out_specs=VMEM,
         scratch_shapes=[
@@ -434,7 +434,7 @@
             collective_id=0, has_side_effects=True, vmem_limit_bytes=56 * 2**20
         ),
         name="whiten",
-    )(comp_sizes, labels.reshape(tiles, LANES), observed)
+    )(comp_sizes, labels.reshape(tiles, LANES), observed).astype(BF16)
 
 
 def solution(mesh):

time: 24.6 us -> 23.1 us (0.939)
  local copies, waits for them, and re-layouts: 1.53 us -> 0 us
  other arithmetic: 0 us -> 0.65 us
  Pallas kernels: 22.8 us -> 22.2 us
    unnamed x1 -> x0, local copies, waits for them, and re-layouts: 1.53 us -> none
    convert_element_type x0 -> x1, other arithmetic: none -> 0.65 us  [body(): return pl.pallas_call(functools.partial(fused_kernel, samples_count, grou...]
    pallas_call x1, Pallas kernels: 22.8 us -> 22.2 us  [body(): pl.pallas_call(functools.partial(fused_kernel, samples_count, groups_coun...]
where the time goes in v1:
time: 23.1 us; the launch traced here: 22.9 us
  Pallas kernels  22.2 us (96%)
  other arithmetic  0.65 us (3%)
    pallas_call x1, Pallas kernels, body(): pl.pallas_call(functools.partial(fused_kernel, samples_count, groups_coun...  22.2 us
    convert_element_type x1, other arithmetic, body(): return pl.pallas_call(functools.partial(fused_kernel, samples_count, grou...  0.65 us

profile of v1, /device:TPU:0, one launch (start us, length us, event | category | flops | bytes accessed | tf_op | source)
XLA Modules:
  0.0 22.9 jit_solution(4746677717000917496)
XLA Ops:
  0.0 22.2 %whiten.1 = f32[16,2560]{1,0:T(8,128)S(1)} custom-call(s32[8]{0:T(128)} %size_hbm.1, s32[20,128]{1,0:T(8,128)} %bitcast.1, bf16[16,2560]{1,0:T(8,128)(2,1)} %observed_hbm.1), custom_call_target="tpu_custom_call" | custom-call | tf_op jit(solution)/shard_map/whiten/pallas_call | solution.py:398
  22.2 0.6 %convert_element_type.3 = bf16[16,2560]{1,0:T(8,128)(2,1)} convert(f32[16,2560]{1,0:T(8,128)S(1)} %whiten.1) | non-fusion elementwise | flops 40960 | bytes 245760 | tf_op jit(solution)/shard_map/convert_element_type | solution.py:437

commit v2 on v1

--- a/solution.py
+++ b/solution.py
@@ -382,11 +382,464 @@
         item.wait_send()
 
 
+def pieces(value):
+    high = value.astype(BF16)
+    return high, (value - high.astype(F32)).astype(BF16)
+
+
+def stack_product(lefts, right):
+    extent = right[0].shape[1]
+    pair = jnp.concatenate(right, axis=1)
+    left = jnp.concatenate([jnp.concatenate(item, axis=1) for item in lefts], axis=0)
+    both = jnp.dot(left, jnp.concatenate([pair, pair], axis=0), preferred_element_type=F32)
+    whole = both[:, extent:] + both[:, :extent]
+    rows = right[0].shape[0]
+    return [whole[i * rows : (i + 1) * rows] for i in range(len(lefts))]
+
+
+def residual_powers(gram, peak):
+    extent = gram.shape[0]
+    one = eye(extent, jnp.ones((1, 1), F32))
+    positive = peak > 0.0
+    unit = jnp.where(positive, 1.0 / jnp.where(positive, peak, 1.0), 0.0)
+    power = {1: one - gram * unit}
+    cut = {1: pieces(power[1])}
+    yield
+
+    def extend(names, by):
+        for name, value in zip(names, stack_product([cut[n - by] for n in names], cut[by])):
+            power[name] = value
+            cut[name] = pieces(value)
+
+    extend([2], 1)
+    yield
+    extend([3, 4], 2)
+    yield
+    extend([5, 6, 7, 8], 4)
+    total = {8: one + sum(power[i] for i in range(1, 8))}
+    first = pieces(total[8])
+    yield
+    power[16], more = stack_product([cut[8], first], cut[8])
+    total[16] = total[8] + more
+    cut[16] = pieces(power[16])
+    yield
+    power[24], more = stack_product([cut[8], first], cut[16])
+    total[24] = total[16] + more
+    yield power, total
+
+
+def residual_series(power, total, e):
+    raised = {0: jnp.ones_like(e), 1: e}
+    for i in (2, 3, 4, 5, 6, 7, 8):
+        raised[i] = raised[i // 2] * raised[i - i // 2]
+    raised[15] = raised[8] * raised[7]
+    raised[16] = raised[8] * raised[8]
+    raised[23] = raised[16] * raised[7]
+    raised[24] = raised[16] * raised[8]
+    tail = {7: raised[7]}
+    for i in range(6, -1, -1):
+        tail[i] = raised[i] + tail[i + 1]
+    eight = tail[0]
+    extent = power[1].shape[0]
+    series = eye(extent, eight - raised[7])
+    for i in range(1, 7):
+        series = series + power[i] * (tail[i] - raised[7])
+    spread = sum(power[i] * raised[i] for i in (8, 16, 24))
+    rest = sum(total[i] * (eight * raised[i - 1]) for i in (8, 16, 24))
+    (through,) = stack_product([pieces(spread)], pieces(series))
+    whole = eight * (1.0 + raised[8]) * (1.0 + raised[16])
+    return through + (series + rest), whole
+
+
+def whiten_pair(block, odd, sizes, same_ref, inverse_ref, wait_average, out):
+    samples, width = block.shape
+    odd_bits = odd.astype(BF16)
+    second = block * odd_bits
+    first = block * (1.0 - odd).astype(BF16)
+    both = jnp.concatenate([first, second], axis=0)
+    both_turned = both.T
+    turned = both_turned[:, :samples] + both_turned[:, samples:]
+    inner = jnp.dot(block, both_turned, preferred_element_type=F32)
+    sums = jnp.zeros((1, width), F32)
+    for r in range(0, width, LANES):
+        part = jnp.dot(both_turned[r : r + LANES], both, preferred_element_type=F32)
+        sums = sums + jnp.sum(jnp.abs(part), axis=0, keepdims=True)
+    peaks = [jnp.max(sums * side, axis=1, keepdims=True) for side in (1.0 - odd, odd)]
+    grams = [inner[:, :samples], inner[:, samples:]]
+    traces = []
+    for gram in grams:
+        kept = gram * eye(samples, jnp.ones((1, 1), F32))
+        traces.append(jnp.sum(jnp.sum(kept, axis=0, keepdims=True), axis=1, keepdims=True))
+    makers = [residual_powers(gram, peak) for gram, peak in zip(grams, peaks)]
+    for _ in range(6):
+        found = [next(maker) for maker in makers]
+    average = wait_average()
+    weight = (1.0 - shrink) / samples
+    middles, wholes, inverse_bounds, factors = [], [], [], []
+    for (power, total), peak, trace, size in zip(found, peaks, traces, sizes):
+        lift = shrink * (trace / samples / size) + ridge * average
+        inverse_bound = 1.0 / (weight * peak + lift)
+        middle, whole = residual_series(power, total, weight * peak * inverse_bound)
+        middles += pieces(middle)
+        wholes.append(whole)
+        inverse_bounds.append(inverse_bound)
+        factors.append(weight * inverse_bound)
+
+    def by_side(values):
+        return jnp.where(odd > 0.5, values[1], values[0])
+
+    mixed = jnp.dot(
+        jnp.concatenate(middles, axis=1),
+        jnp.concatenate([first, first, second, second], axis=0),
+        preferred_element_type=F32,
+    )
+    mixed = mixed * (-by_side(factors))
+    stacked = jnp.concatenate(pieces(mixed), axis=0)
+    scale = by_side(inverse_bounds)
+    peak_line = by_side(wholes)
+    wide_turned = jnp.concatenate([turned, turned], axis=1)
+    for r in range(0, width, LANES):
+        part = jnp.dot(wide_turned[r : r + LANES], stacked, preferred_element_type=F32)
+        line = eye(LANES, jnp.ones((1, 1), F32)) * peak_line[:, r : r + LANES]
+        for q in range(0, width, LANES):
+            value = part[:, q : q + LANES]
+            if q == r:
+                value = value + line
+            value = (value * scale[:, q : q + LANES]).astype(BF16)
+            inverse_ref[r : r + LANES, q : q + LANES] = value * same_ref[r : r + LANES, q : q + LANES]
+    out(jnp.dot(block, inverse_ref[...], preferred_element_type=F32).astype(BF16))
+
+
+def pair_kernel(
+    samples_count,
+    groups_count,
+    entries,
+    size_hbm,
+    label_hbm,
+    observed_hbm,
+    result_ref,
+    size_ref,
+    label_ref,
+    observed_ref,
+    load_sem,
+    sorted_ref,
+    side_ref,
+    high_ref,
+    turn_ref,
+    place_ref,
+    packed_ref,
+    held_ref,
+    odd_ref,
+    same_ref,
+    inverse_ref,
+    done_ref,
+    back_ref,
+    energy_ref,
+    all_ref,
+    total_ref,
+    total_in_ref,
+    energy_send,
+    energy_recv,
+    total_send,
+    total_recv,
+    out_send,
+    out_recv,
+    back_send,
+    back_recv,
+):
+    me = lax.axis_index("samples")
+    group = lax.axis_index("groups")
+    pairs, rows, width = packed_ref.shape
+    tiles = sorted_ref.shape[0]
+    table_rows = high_ref.shape[1]
+    parts = width // LANES
+    opening = samples_count // 4
+    mine = jnp.clip(me - opening, 0, pairs - 1)
+    inverts = (me >= opening) & (me < opening + pairs)
+    odd_group = lax.rem(group, 2)
+    number = group * samples_count + me
+    devices = samples_count * groups_count
+
+    def copy(source, target, send, recv, sample, other):
+        return pltpu.make_async_remote_copy(
+            src_ref=source,
+            dst_ref=target,
+            send_sem=send,
+            recv_sem=recv,
+            device_id=(sample, other),
+            device_id_type=MESH,
+        )
+
+    def signal(sample, other):
+        pl.semaphore_signal(barrier, inc=1, device_id=(sample, other), device_id_type=MESH)
+
+    loads = [
+        pltpu.make_async_copy(source, target, load_sem.at[i])
+        for i, (source, target) in enumerate(
+            ((label_hbm, label_ref), (observed_hbm, observed_ref), (size_hbm, size_ref))
+        )
+    ]
+    for item in loads:
+        item.start()
+    barrier = pltpu.get_barrier_semaphore()
+
+    @pl.when(inverts)
+    def _():
+        for k in range(1, samples_count):
+            signal(lax.rem(me + k, samples_count), group)
+
+    @pl.when(inverts & (odd_group == 0))
+    def _():
+        for j in range(1, groups_count):
+            for k in range(samples_count):
+                signal(lax.rem(me + k, samples_count), lax.rem(group + j, groups_count))
+
+    for item in loads:
+        item.wait()
+
+    slots = 2 * pairs
+    first = group * slots
+    slot = lax.broadcasted_iota(jnp.int32, (table_rows, LANES), 0)
+    down = lax.broadcasted_iota(jnp.int32, (LANES, LANES), 0)
+    across = lax.broadcasted_iota(jnp.int32, (LANES, LANES), 1)
+    upto = (down <= across).astype(BF16)
+    ones = jnp.ones((LANES, LANES), BF16)
+    energy = jnp.zeros((8, LANES), F32)
+    equals, lesses, blocks, sides = [], [], [], []
+    for t in range(tiles):
+        block = observed_ref[:, t * LANES : (t + 1) * LANES]
+        wide = block.astype(F32)
+        square = wide * wide
+        for r in range(0, rows, 8):
+            energy = energy + square[r : r + 8]
+        label = label_ref[pl.ds(t, 1), :] - first
+        pair = label >> 1
+        equals.append((pair == slot).astype(F32))
+        lesses.append((pair < slot).astype(F32))
+        side = jnp.broadcast_to((label & 1).astype(F32), (rows, LANES)).astype(BF16)
+        blocks.append(jnp.concatenate([block, side], axis=0))
+    energy_ref[0] = jnp.sum(energy, axis=0, keepdims=True)
+    all_ref[number] = energy_ref[0]
+    equal_all = jnp.concatenate(equals, axis=0).astype(BF16)
+    less_all = jnp.concatenate(lesses, axis=0).astype(BF16)
+    ranks = jnp.dot(equal_all, upto, preferred_element_type=F32) - 1.0
+    counts = jnp.dot(equal_all, ones, preferred_element_type=F32)
+    befores = jnp.dot(less_all, ones, preferred_element_type=F32)
+    base = jnp.zeros((table_rows, LANES), F32)
+    for t in range(tiles):
+        span = slice(t * table_rows, (t + 1) * table_rows)
+        rank, count, before, equal = ranks[span], counts[span], befores[span], equals[t]
+        local = jnp.sum(equal * (before + rank), axis=0, keepdims=True).astype(jnp.int32)
+        whole = slot.astype(F32) * width + base + rank
+        place_ref[pl.ds(t, 1), :] = jnp.sum(equal * whole, axis=0, keepdims=True).astype(jnp.int32)
+        choose = (down == local).astype(BF16)
+        ordered = lax.dot_general(blocks[t], choose, (((1,), (1,)), ((), ())), preferred_element_type=F32)
+        sorted_ref[t] = ordered[:rows]
+        side_ref[t] = ordered[rows : rows + 8]
+        high_ref[t] = (base + count).astype(jnp.int32)
+        turn_ref[t] = (before - base).astype(jnp.int32)
+        base = base + count
+
+    lane = lax.broadcasted_iota(jnp.int32, (rows, LANES), 1)
+
+    def reach(t):
+        return range(max(0, parts - tiles + t), min(parts, t + 1))
+
+    def pack(c, source, height):
+        packed = [jnp.zeros((height, LANES), F32)] * parts
+        place = lane[:height]
+        for t in reversed(range(tiles)):
+            high = jnp.broadcast_to(high_ref[t, pl.ds(c, 1), :], (height, LANES))
+            turn = jnp.broadcast_to(turn_ref[t, pl.ds(c, 1), :], (height, LANES))
+            moved = lane_gather(source[t], (place + turn) & (LANES - 1))
+            for q in reach(t):
+                packed[q] = jnp.where(place + q * LANES < high, moved, packed[q])
+        return packed
+
+    for p in range(pairs):
+        for q, value in enumerate(pack(p, sorted_ref, rows)):
+            packed_ref[p, :, q * LANES : (q + 1) * LANES] = value.astype(BF16)
+
+    out_copies = [
+        copy(packed_ref.at[p], held_ref.at[me], out_send.at[p], out_recv.at[me], opening + p, group)
+        for p in range(pairs)
+    ]
+    hubs = [(opening + p, g) for g in range(0, groups_count, 2) for p in range(pairs)]
+    energy_copies = [
+        copy(energy_ref.at[0], all_ref.at[number], energy_send.at[i], energy_recv, sample, other)
+        for i, (sample, other) in enumerate(hubs)
+    ]
+
+    def elsewhere(sample, other=None):
+        away = me != sample
+        return away if other is None else away | (group != other)
+
+    pl.semaphore_wait(barrier, len(hubs) + odd_group * pairs - inverts.astype(jnp.int32))
+    for item, hub in zip(energy_copies, hubs):
+        pl.when(elsewhere(*hub))(item.start)
+    for p, item in enumerate(out_copies):
+        pl.when(elsewhere(opening + p))(item.start)
+
+    total_copy = copy(total_ref, total_in_ref, total_send, total_recv, me, lax.rem(group + 1, groups_count))
+
+    @pl.when(inverts)
+    def _():
+        held_ref[me] = packed_ref[mine]
+        odd = jnp.concatenate(pack(mine, side_ref, 8), axis=1)
+        odd_ref[...] = odd
+        odd_turned = jnp.concatenate([odd] * (LANES // 8), axis=0).T
+        for r in range(0, width, LANES):
+            for q in range(0, width, LANES):
+                same = odd_turned[r : r + LANES] == jnp.broadcast_to(odd[:1, q : q + LANES], (LANES, LANES))
+                same_ref[r : r + LANES, q : q + LANES] = same.astype(F32).astype(BF16)
+        for k in range(1, samples_count):
+            other = lax.rem(me + k, samples_count)
+            copy(
+                packed_ref.at[0], held_ref.at[other], out_send.at[0], out_recv.at[other], me, group
+            ).wait_recv()
+
+        def wait_average():
+            @pl.when(odd_group == 0)
+            def _():
+                rest = all_ref.at[pl.ds(0, devices - 1)]
+                copy(rest, rest, energy_send.at[0], energy_recv, me, group).wait_recv()
+                total_in_ref[...] = jnp.sum(all_ref[...], axis=0)
+                total_ref[...] = jnp.sum(all_ref[...], axis=0)
+                total_copy.start()
+
+            @pl.when(odd_group == 1)
+            def _():
+                total_copy.wait_recv()
+
+            return jnp.sum(total_in_ref[...], axis=1, keepdims=True) / entries
+
+        def out(value):
+            done_ref[...] = value.reshape(samples_count, rows, width)
+
+        sizes = [
+            jnp.full((1, 1), size_ref[2 * mine + h], jnp.int32).astype(F32) for h in range(2)
+        ]
+        block = held_ref[...].reshape(samples_count * rows, width)
+        whiten_pair(block, odd_ref[:1], sizes, same_ref, inverse_ref, wait_average, out)
+        for k in range(1, samples_count):
+            other = lax.rem(me + k, samples_count)
+            copy(
+                done_ref.at[other], back_ref.at[mine], back_send.at[k - 1], back_recv.at[mine], other, group
+            ).start()
+        back_ref[mine] = done_ref[me]
+
+    for k in range(pairs):
+        p = jnp.where(me < opening + pairs // 2, k, pairs - 1 - k)
+
+        @pl.when(elsewhere(opening + p))
+        def _():
+            copy(
+                done_ref.at[0], back_ref.at[p], back_send.at[0], back_recv.at[p], opening + p, group
+            ).wait_recv()
+
+        wide = [back_ref[p, :, q * LANES : (q + 1) * LANES].astype(F32) for q in range(parts)]
+        for t in range(tiles):
+            place = jnp.broadcast_to(place_ref[pl.ds(t, 1), :], (rows, LANES))
+            index = place & (LANES - 1)
+            tile = (place >> (LANES.bit_length() - 1)) - p * parts
+            if k == 0:
+                value = jnp.zeros((rows, LANES), F32)
+            else:
+                value = result_ref[:, t * LANES : (t + 1) * LANES]
+            for q in reach(t):
+                value = jnp.where(tile == q, lane_gather(wide[q], index), value)
+            result_ref[:, t * LANES : (t + 1) * LANES] = value
+
+    for item, hub in zip(energy_copies, hubs):
+        pl.when(elsewhere(*hub))(item.wait_send)
+    for p, item in enumerate(out_copies):
+        pl.when(elsewhere(opening + p))(item.wait_send)
+    pl.when(inverts & (odd_group == 0))(total_copy.wait_send)
+
+    @pl.when(inverts)
+    def _():
+        for k in range(1, samples_count):
+            other = lax.rem(me + k, samples_count)
+            copy(
+                done_ref.at[other], back_ref.at[mine], back_send.at[k - 1], back_recv.at[mine], other, group
+            ).wait_send()
+
+
+def paired(observed, labels, comp_sizes, samples_count, groups_count):
+    rows, width = observed.shape
+    pairs = comp_sizes.shape[0] // 2
+    pair_width = width // pairs
+    tiles = width // LANES
+    devices = samples_count * groups_count
+    table_rows = -(-pairs // 8) * 8
+    kind = pltpu.SemaphoreType.DMA
+    table = pltpu.VMEM((tiles, table_rows, LANES), jnp.int32)
+    square = pltpu.VMEM((pair_width, pair_width), BF16)
+    blocks = pltpu.VMEM((samples_count, rows, pair_width), BF16)
+    kept = pltpu.VMEM((pairs, rows, pair_width), BF16)
+    line = pltpu.VMEM((1, LANES), F32)
+    return pl.pallas_call(
+        functools.partial(
+            pair_kernel, samples_count, groups_count, float(samples_count * rows * width * groups_count)
+        ),
+        out_shape=pltpu.VMEM((rows, width), F32),
+        in_specs=[pl.BlockSpec(memory_space=pltpu.HBM)] * 3,
+        out_specs=VMEM,
+        scratch_shapes=[
+            pltpu.SMEM(comp_sizes.shape, jnp.int32),
+            pltpu.VMEM((tiles, LANES), jnp.int32),
+            pltpu.VMEM((rows, width), BF16),
+            kind((3,)),
+            pltpu.VMEM((tiles, rows, LANES), F32),
+            pltpu.VMEM((tiles, 8, LANES), F32),
+            table,
+            table,
+            pltpu.VMEM((tiles, LANES), jnp.int32),
+            kept,
+            blocks,
+            pltpu.VMEM((8, pair_width), F32),
+            square,
+            square,
+            blocks,
+            kept,
+            pltpu.VMEM((1, 1, LANES), F32),
+            pltpu.VMEM((devices, 1, LANES), F32),
+            line,
+            line,
+            kind((pairs * groups_count // 2,)),
+            kind,
+            kind,
+            kind,
+            kind((pairs,)),
+            kind((samples_count,)),
+            kind((samples_count,)),
+            kind((pairs,)),
+        ],
+        compiler_params=pltpu.CompilerParams(
+            collective_id=0, has_side_effects=True, vmem_limit_bytes=56 * 2**20
+        ),
+        name="whiten",
+    )(comp_sizes, labels.reshape(tiles, LANES), observed).astype(BF16)
+
+
+def pairs_fit(rows, width, slots, samples_count, groups_count):
+    return (
+        slots == samples_count
+        and samples_count % 4 == 0
+        and groups_count % 2 == 0
+        and rows * samples_count < CMAX
+        and (2 * width // slots) % LANES == 0
+        and rows % 16 == 0
+    )
+
+
 def body(observed, labels, comp_sizes):
     rows, width = observed.shape
     slots = comp_sizes.shape[0]
     samples_count = lax.axis_size("samples")
     groups_count = lax.axis_size("groups")
+    if pairs_fit(rows, width, slots, samples_count, groups_count):
+        return paired(observed, labels, comp_sizes, samples_count, groups_count)
     slot_here = slots // samples_count
     tiles = width // LANES
     samples = rows * samples_count

time: 23.1 us -> 18.9 us (0.82)
  the two profiles are of different devices: /device:TPU:0 before, /device:TPU:1 now
where the time goes in v2:
time: 18.9 us; the launch traced here: 18.7 us
  Pallas kernels  18 us (95%)
  other arithmetic  0.65 us (3%)
    pallas_call x1, Pallas kernels, paired(): pl.pallas_call(functools.partial(pair_kernel, samples_count, groups_count...  18 us
    convert_element_type x1, other arithmetic, paired(): return pl.pallas_call(functools.partial(pair_kernel, samples_count, group...  0.65 us

profile of v2, /device:TPU:1, one launch (start us, length us, event | category | flops | bytes accessed | tf_op | source)
XLA Modules:
  0.0 18.7 jit_solution(7555532263802429461)
XLA Ops:
  0.0 18.0 %whiten.1 = f32[16,2560]{1,0:T(8,128)S(1)} custom-call(s32[8]{0:T(128)} %size_hbm.1, s32[20,128]{1,0:T(8,128)} %bitcast.1, bf16[16,2560]{1,0:T(8,128)(2,1)} %observed_hbm.1), custom_call_target="tpu_custom_call" | custom-call | tf_op jit(solution)/shard_map/whiten/pallas_call | solution.py:781
  18.0 0.6 %convert_element_type.3 = bf16[16,2560]{1,0:T(8,128)(2,1)} convert(f32[16,2560]{1,0:T(8,128)S(1)} %whiten.1) | non-fusion elementwise | flops 40960 | bytes 245760 | tf_op jit(solution)/shard_map/convert_element_type | solution.py:822

commit v3 on v2

--- a/solution.py
+++ b/solution.py
@@ -397,61 +397,39 @@
     return [whole[i * rows : (i + 1) * rows] for i in range(len(lefts))]
 
 
-def residual_powers(gram, peak):
+def residual_series(gram, peak, box):
     extent = gram.shape[0]
     one = eye(extent, jnp.ones((1, 1), F32))
     positive = peak > 0.0
     unit = jnp.where(positive, 1.0 / jnp.where(positive, peak, 1.0), 0.0)
-    power = {1: one - gram * unit}
-    cut = {1: pieces(power[1])}
+    first = one - gram * unit
+    cut = pieces(first)
+    (second,) = stack_product([cut], cut)
+    cut_second = pieces(second)
     yield
-
-    def extend(names, by):
-        for name, value in zip(names, stack_product([cut[n - by] for n in names], cut[by])):
-            power[name] = value
-            cut[name] = pieces(value)
-
-    extend([2], 1)
+    third, power = stack_product([cut, cut_second], cut_second)
     yield
-    extend([3, 4], 2)
+    e = box[0]
+    square = e * e
+    count = 1.0 + e
+    series = one * (count + square) + first * (e + square) + second * square
+    total = (one + first) + (second + third)
+    count = count * (1.0 + square)
+    before, raised = e * square, square * square
     yield
-    extend([5, 6, 7, 8], 4)
-    total = {8: one + sum(power[i] for i in range(1, 8))}
-    first = pieces(total[8])
-    yield
-    power[16], more = stack_product([cut[8], first], cut[8])
-    total[16] = total[8] + more
-    cut[16] = pieces(power[16])
-    yield
-    power[24], more = stack_product([cut[8], first], cut[16])
-    total[24] = total[16] + more
-    yield power, total
-
-
-def residual_series(power, total, e):
-    raised = {0: jnp.ones_like(e), 1: e}
-    for i in (2, 3, 4, 5, 6, 7, 8):
-        raised[i] = raised[i // 2] * raised[i - i // 2]
-    raised[15] = raised[8] * raised[7]
-    raised[16] = raised[8] * raised[8]
-    raised[23] = raised[16] * raised[7]
-    raised[24] = raised[16] * raised[8]
-    tail = {7: raised[7]}
-    for i in range(6, -1, -1):
-        tail[i] = raised[i] + tail[i + 1]
-    eight = tail[0]
-    extent = power[1].shape[0]
-    series = eye(extent, eight - raised[7])
-    for i in range(1, 7):
-        series = series + power[i] * (tail[i] - raised[7])
-    spread = sum(power[i] * raised[i] for i in (8, 16, 24))
-    rest = sum(total[i] * (eight * raised[i - 1]) for i in (8, 16, 24))
-    (through,) = stack_product([pieces(spread)], pieces(series))
-    whole = eight * (1.0 + raised[8]) * (1.0 + raised[16])
-    return through + (series + rest), whole
-
-
-def whiten_pair(block, odd, sizes, same_ref, inverse_ref, wait_average, out):
+    for _ in range(2):
+        cut = pieces(power)
+        power, through, more = stack_product([cut, pieces(series), pieces(total)], cut)
+        series = series + through * raised + total * (before * count)
+        total = total + more
+        count = count * (1.0 + raised)
+        before, raised = before * raised, raised * raised
+        yield
+    (through,) = stack_product([pieces(series)], pieces(power))
+    yield series + through * raised + total * (before * count), count * (1.0 + raised)
+
+
+def whiten_pair(block, odd, sizes, same_ref, inverse_ref, share_total, wait_average, out):
     samples, width = block.shape
     odd_bits = odd.astype(BF16)
     second = block * odd_bits
@@ -470,20 +448,25 @@
     for gram in grams:
         kept = gram * eye(samples, jnp.ones((1, 1), F32))
         traces.append(jnp.sum(jnp.sum(kept, axis=0, keepdims=True), axis=1, keepdims=True))
-    makers = [residual_powers(gram, peak) for gram, peak in zip(grams, peaks)]
-    for _ in range(6):
-        found = [next(maker) for maker in makers]
+    share_total()
+    boxes = [[], []]
+    makers = [residual_series(gram, peak, box) for gram, peak, box in zip(grams, peaks, boxes)]
+    for _ in range(2):
+        for maker in makers:
+            next(maker)
     average = wait_average()
     weight = (1.0 - shrink) / samples
-    middles, wholes, inverse_bounds, factors = [], [], [], []
-    for (power, total), peak, trace, size in zip(found, peaks, traces, sizes):
+    inverse_bounds = []
+    for peak, trace, size, box in zip(peaks, traces, sizes, boxes):
         lift = shrink * (trace / samples / size) + ridge * average
         inverse_bound = 1.0 / (weight * peak + lift)
-        middle, whole = residual_series(power, total, weight * peak * inverse_bound)
-        middles += pieces(middle)
-        wholes.append(whole)
+        box.append(weight * peak * inverse_bound)
         inverse_bounds.append(inverse_bound)
-        factors.append(weight * inverse_bound)
+    for _ in range(4):
+        found = [next(maker) for maker in makers]
+    middles = [piece for middle, _ in found for piece in pieces(middle)]
+    wholes = [whole for _, whole in found]
+    factors = [weight * inverse_bound for inverse_bound in inverse_bounds]
 
     def by_side(values):
         return jnp.where(odd > 0.5, values[1], values[0])
@@ -556,7 +539,8 @@
     opening = samples_count // 4
     mine = jnp.clip(me - opening, 0, pairs - 1)
     inverts = (me >= opening) & (me < opening + pairs)
-    odd_group = lax.rem(group, 2)
+    hub_group = group == 0
+    later = jnp.minimum(group, 1)
     number = group * samples_count + me
     devices = samples_count * groups_count
 
@@ -588,7 +572,7 @@
         for k in range(1, samples_count):
             signal(lax.rem(me + k, samples_count), group)
 
-    @pl.when(inverts & (odd_group == 0))
+    @pl.when(inverts & hub_group)
     def _():
         for j in range(1, groups_count):
             for k in range(samples_count):
@@ -664,7 +648,7 @@
         copy(packed_ref.at[p], held_ref.at[me], out_send.at[p], out_recv.at[me], opening + p, group)
         for p in range(pairs)
     ]
-    hubs = [(opening + p, g) for g in range(0, groups_count, 2) for p in range(pairs)]
+    hubs = [(opening + p, 0) for p in range(pairs)]
     energy_copies = [
         copy(energy_ref.at[0], all_ref.at[number], energy_send.at[i], energy_recv, sample, other)
         for i, (sample, other) in enumerate(hubs)
@@ -674,13 +658,15 @@
         away = me != sample
         return away if other is None else away | (group != other)
 
-    pl.semaphore_wait(barrier, len(hubs) + odd_group * pairs - inverts.astype(jnp.int32))
+    pl.semaphore_wait(barrier, (1 + later) * pairs - inverts.astype(jnp.int32))
     for item, hub in zip(energy_copies, hubs):
         pl.when(elsewhere(*hub))(item.start)
     for p, item in enumerate(out_copies):
         pl.when(elsewhere(opening + p))(item.start)
 
-    total_copy = copy(total_ref, total_in_ref, total_send, total_recv, me, lax.rem(group + 1, groups_count))
+    total_copies = [
+        copy(total_ref, total_in_ref, total_send.at[g - 1], total_recv, me, g) for g in range(1, groups_count)
+    ]
 
     @pl.when(inverts)
     def _():
@@ -698,18 +684,20 @@
                 packed_ref.at[0], held_ref.at[other], out_send.at[0], out_recv.at[other], me, group
             ).wait_recv()
 
-        def wait_average():
-            @pl.when(odd_group == 0)
+        def share_total():
+            @pl.when(hub_group)
             def _():
                 rest = all_ref.at[pl.ds(0, devices - 1)]
                 copy(rest, rest, energy_send.at[0], energy_recv, me, group).wait_recv()
                 total_in_ref[...] = jnp.sum(all_ref[...], axis=0)
                 total_ref[...] = jnp.sum(all_ref[...], axis=0)
-                total_copy.start()
-
-            @pl.when(odd_group == 1)
+                for item in total_copies:
+                    item.start()
+
+        def wait_average():
+            @pl.when(group != 0)
             def _():
-                total_copy.wait_recv()
+                total_copies[0].wait_recv()
 
             return jnp.sum(total_in_ref[...], axis=1, keepdims=True) / entries
 
@@ -720,7 +708,7 @@
             jnp.full((1, 1), size_ref[2 * mine + h], jnp.int32).astype(F32) for h in range(2)
         ]
         block = held_ref[...].reshape(samples_count * rows, width)
-        whiten_pair(block, odd_ref[:1], sizes, same_ref, inverse_ref, wait_average, out)
+        whiten_pair(block, odd_ref[:1], sizes, same_ref, inverse_ref, share_total, wait_average, out)
         for k in range(1, samples_count):
             other = lax.rem(me + k, samples_count)
             copy(
@@ -754,7 +742,12 @@
         pl.when(elsewhere(*hub))(item.wait_send)
     for p, item in enumerate(out_copies):
         pl.when(elsewhere(opening + p))(item.wait_send)
-    pl.when(inverts & (odd_group == 0))(total_copy.wait_send)
+
+    @pl.when(inverts & hub_group)
+    def _():
+        for item in total_copies:
+            item.wait_send()
+
 
     @pl.when(inverts)
     def _():
@@ -806,9 +799,9 @@
             pltpu.VMEM((devices, 1, LANES), F32),
             line,
             line,
-            kind((pairs * groups_count // 2,)),
+            kind((pairs,)),
             kind,
-            kind,
+            kind((groups_count - 1,)),
             kind,
             kind((pairs,)),
             kind((samples_count,)),
@@ -826,7 +819,7 @@
     return (
         slots == samples_count
         and samples_count % 4 == 0
-        and groups_count % 2 == 0
+        and groups_count > 1
         and rows * samples_count < CMAX
         and (2 * width // slots) % LANES == 0
         and rows % 16 == 0

time: 18.9 us -> 17.5 us (0.926)
  the two profiles are of different devices: /device:TPU:1 before, /device:TPU:2 now
where the time goes in v3:
time: 17.5 us; the launch traced here: 17.3 us
  Pallas kernels  16.6 us (95%)
  other arithmetic  0.65 us (4%)
    pallas_call x1, Pallas kernels, paired(): pl.pallas_call(functools.partial(pair_kernel, samples_count, groups_count...  16.6 us
    convert_element_type x1, other arithmetic, paired(): return pl.pallas_call(functools.partial(pair_kernel, samples_count, group...  0.65 us

profile of v3, /device:TPU:2, one launch (start us, length us, event | category | flops | bytes accessed | tf_op | source)
XLA Modules:
  0.0 17.3 jit_solution(11477450423915162994)
XLA Ops:
  0.0 16.6 %whiten.1 = f32[16,2560]{1,0:T(8,128)S(1)} custom-call(s32[8]{0:T(128)} %size_hbm.1, s32[20,128]{1,0:T(8,128)} %bitcast.1, bf16[16,2560]{1,0:T(8,128)(2,1)} %observed_hbm.1), custom_call_target="tpu_custom_call" | custom-call | tf_op jit(solution)/shard_map/whiten/pallas_call | solution.py:774
  16.7 0.6 %convert_element_type.3 = bf16[16,2560]{1,0:T(8,128)(2,1)} convert(f32[16,2560]{1,0:T(8,128)S(1)} %whiten.1) | non-fusion elementwise | flops 40960 | bytes 245760 | tf_op jit(solution)/shard_map/convert_element_type | solution.py:815

commit v4 on v3

--- a/solution.py
+++ b/solution.py
@@ -429,31 +429,103 @@
     yield series + through * raised + total * (before * count), count * (1.0 + raised)
 
 
-def whiten_pair(block, odd, sizes, same_ref, inverse_ref, share_total, wait_average, out):
+def residual_powers(gram, peak):
+    extent = gram.shape[0]
+    one = eye(extent, jnp.ones((1, 1), F32))
+    positive = peak > 0.0
+    unit = jnp.where(positive, 1.0 / jnp.where(positive, peak, 1.0), 0.0)
+    power = {1: one - gram * unit}
+    cut = {1: pieces(power[1])}
+    yield
+
+    def extend(names, by):
+        for name, value in zip(names, stack_product([cut[n - by] for n in names], cut[by])):
+            power[name] = value
+            cut[name] = pieces(value)
+
+    extend([2], 1)
+    yield
+    extend([3, 4], 2)
+    yield
+    extend([5, 6, 7, 8], 4)
+    total = {8: one + sum(power[i] for i in range(1, 8))}
+    first = pieces(total[8])
+    yield
+    power[16], more = stack_product([cut[8], first], cut[8])
+    total[16] = total[8] + more
+    cut[16] = pieces(power[16])
+    yield
+    power[24], more = stack_product([cut[8], first], cut[16])
+    total[24] = total[16] + more
+    yield power, total
+
+
+def powers_series(power, total, e):
+    raised = {0: jnp.ones_like(e), 1: e}
+    for i in (2, 3, 4, 5, 6, 7, 8):
+        raised[i] = raised[i // 2] * raised[i - i // 2]
+    raised[15] = raised[8] * raised[7]
+    raised[16] = raised[8] * raised[8]
+    raised[23] = raised[16] * raised[7]
+    raised[24] = raised[16] * raised[8]
+    tail = {7: raised[7]}
+    for i in range(6, -1, -1):
+        tail[i] = raised[i] + tail[i + 1]
+    eight = tail[0]
+    extent = power[1].shape[0]
+    series = eye(extent, eight - raised[7])
+    for i in range(1, 7):
+        series = series + power[i] * (tail[i] - raised[7])
+    spread = sum(power[i] * raised[i] for i in (8, 16, 24))
+    rest = sum(total[i] * (eight * raised[i - 1]) for i in (8, 16, 24))
+    (through,) = stack_product([pieces(spread)], pieces(series))
+    whole = eight * (1.0 + raised[8]) * (1.0 + raised[16])
+    return through + (series + rest), whole
+
+
+def late_series(gram, peak, box):
+    maker = residual_powers(gram, peak)
+    for _ in range(5):
+        next(maker)
+        yield
+    power, total = next(maker)
+    yield
+    yield powers_series(power, total, box[0])
+
+
+def whiten_pair(leads, block, odd, sizes, flag_ref, same_ref, inverse_ref, share_total, wait_average, out):
     samples, width = block.shape
-    odd_bits = odd.astype(BF16)
-    second = block * odd_bits
-    first = block * (1.0 - odd).astype(BF16)
+    turned = block.T
+    second = block * odd.astype(BF16)
+    first = block - second
     both = jnp.concatenate([first, second], axis=0)
-    both_turned = both.T
-    turned = both_turned[:, :samples] + both_turned[:, samples:]
+    second_turned = turned * flag_ref[...]
+    both_turned = jnp.concatenate([turned - second_turned, second_turned], axis=1)
     inner = jnp.dot(block, both_turned, preferred_element_type=F32)
-    sums = jnp.zeros((1, width), F32)
+    lines = [jnp.zeros((1, LANES), F32)] * (width // LANES)
     for r in range(0, width, LANES):
-        part = jnp.dot(both_turned[r : r + LANES], both, preferred_element_type=F32)
-        sums = sums + jnp.sum(jnp.abs(part), axis=0, keepdims=True)
+        part = jnp.abs(jnp.dot(both_turned[r : r + LANES], both[:, r:], preferred_element_type=F32))
+        down = jnp.sum(part, axis=0, keepdims=True)
+        for q in range(r, width, LANES):
+            lines[q // LANES] = lines[q // LANES] + down[:, q - r : q - r + LANES]
+        if r + LANES < width:
+            right = sum(part[:, q - r : q - r + LANES] for q in range(r + LANES, width, LANES))
+            lines[r // LANES] = lines[r // LANES] + jnp.sum(right.T, axis=0, keepdims=True)
+    sums = jnp.concatenate(lines, axis=1)
     peaks = [jnp.max(sums * side, axis=1, keepdims=True) for side in (1.0 - odd, odd)]
     grams = [inner[:, :samples], inner[:, samples:]]
     traces = []
     for gram in grams:
         kept = gram * eye(samples, jnp.ones((1, 1), F32))
         traces.append(jnp.sum(jnp.sum(kept, axis=0, keepdims=True), axis=1, keepdims=True))
-    share_total()
     boxes = [[], []]
-    makers = [residual_series(gram, peak, box) for gram, peak, box in zip(grams, peaks, boxes)]
-    for _ in range(2):
+    make = residual_series if leads else late_series
+    makers = [make(gram, peak, box) for gram, peak, box in zip(grams, peaks, boxes)]
+    for step in range(2 if leads else 6):
         for maker in makers:
             next(maker)
+        if leads and step == 0:
+            share_total()
     average = wait_average()
     weight = (1.0 - shrink) / samples
     inverse_bounds = []
@@ -462,7 +534,7 @@
         inverse_bound = 1.0 / (weight * peak + lift)
         box.append(weight * peak * inverse_bound)
         inverse_bounds.append(inverse_bound)
-    for _ in range(4):
+    for _ in range(4 if leads else 1):
         found = [next(maker) for maker in makers]
     middles = [piece for middle, _ in found for piece in pieces(middle)]
     wholes = [whole for _, whole in found]
@@ -482,14 +554,17 @@
     peak_line = by_side(wholes)
     wide_turned = jnp.concatenate([turned, turned], axis=1)
     for r in range(0, width, LANES):
-        part = jnp.dot(wide_turned[r : r + LANES], stacked, preferred_element_type=F32)
+        part = jnp.dot(wide_turned[r : r + LANES], stacked[:, r:], preferred_element_type=F32)
         line = eye(LANES, jnp.ones((1, 1), F32)) * peak_line[:, r : r + LANES]
-        for q in range(0, width, LANES):
-            value = part[:, q : q + LANES]
+        for q in range(r, width, LANES):
+            value = part[:, q - r : q - r + LANES]
             if q == r:
                 value = value + line
             value = (value * scale[:, q : q + LANES]).astype(BF16)
-            inverse_ref[r : r + LANES, q : q + LANES] = value * same_ref[r : r + LANES, q : q + LANES]
+            value = value * same_ref[r : r + LANES, q : q + LANES]
+            inverse_ref[r : r + LANES, q : q + LANES] = value
+            if q > r:
+                inverse_ref[q : q + LANES, r : r + LANES] = value.T
     out(jnp.dot(block, inverse_ref[...], preferred_element_type=F32).astype(BF16))
 
 
@@ -513,6 +588,7 @@
     packed_ref,
     held_ref,
     odd_ref,
+    flag_ref,
     same_ref,
     inverse_ref,
     done_ref,
@@ -644,9 +720,11 @@
         for q, value in enumerate(pack(p, sorted_ref, rows)):
             packed_ref[p, :, q * LANES : (q + 1) * LANES] = value.astype(BF16)
 
+    near_half = me < opening + pairs // 2
+    far_first = [jnp.where(near_half, pairs - 1 - k, k) for k in range(pairs)]
     out_copies = [
-        copy(packed_ref.at[p], held_ref.at[me], out_send.at[p], out_recv.at[me], opening + p, group)
-        for p in range(pairs)
+        copy(packed_ref.at[p], held_ref.at[me], out_send.at[k], out_recv.at[me], opening + p, group)
+        for k, p in enumerate(far_first)
     ]
     hubs = [(opening + p, 0) for p in range(pairs)]
     energy_copies = [
@@ -661,7 +739,7 @@
     pl.semaphore_wait(barrier, (1 + later) * pairs - inverts.astype(jnp.int32))
     for item, hub in zip(energy_copies, hubs):
         pl.when(elsewhere(*hub))(item.start)
-    for p, item in enumerate(out_copies):
+    for p, item in zip(far_first, out_copies):
         pl.when(elsewhere(opening + p))(item.start)
 
     total_copies = [
@@ -674,6 +752,7 @@
         odd = jnp.concatenate(pack(mine, side_ref, 8), axis=1)
         odd_ref[...] = odd
         odd_turned = jnp.concatenate([odd] * (LANES // 8), axis=0).T
+        flag_ref[...] = odd_turned.astype(BF16)
         for r in range(0, width, LANES):
             for q in range(0, width, LANES):
                 same = odd_turned[r : r + LANES] == jnp.broadcast_to(odd[:1, q : q + LANES], (LANES, LANES))
@@ -685,20 +764,17 @@
             ).wait_recv()
 
         def share_total():
-            @pl.when(hub_group)
-            def _():
-                rest = all_ref.at[pl.ds(0, devices - 1)]
-                copy(rest, rest, energy_send.at[0], energy_recv, me, group).wait_recv()
-                total_in_ref[...] = jnp.sum(all_ref[...], axis=0)
-                total_ref[...] = jnp.sum(all_ref[...], axis=0)
-                for item in total_copies:
-                    item.start()
-
-        def wait_average():
-            @pl.when(group != 0)
-            def _():
+            rest = all_ref.at[pl.ds(0, devices - 1)]
+            copy(rest, rest, energy_send.at[0], energy_recv, me, group).wait_recv()
+            total = jnp.sum(all_ref[...], axis=0)
+            total_in_ref[...] = total
+            total_ref[...] = total
+            for item in total_copies:
+                item.start()
+
+        def wait_average(leads):
+            if not leads:
                 total_copies[0].wait_recv()
-
             return jnp.sum(total_in_ref[...], axis=1, keepdims=True) / entries
 
         def out(value):
@@ -707,8 +783,23 @@
         sizes = [
             jnp.full((1, 1), size_ref[2 * mine + h], jnp.int32).astype(F32) for h in range(2)
         ]
-        block = held_ref[...].reshape(samples_count * rows, width)
-        whiten_pair(block, odd_ref[:1], sizes, same_ref, inverse_ref, share_total, wait_average, out)
+        def invert(leads):
+            block = held_ref[...].reshape(samples_count * rows, width)
+            whiten_pair(
+                leads,
+                block,
+                odd_ref[:1],
+                sizes,
+                flag_ref,
+                same_ref,
+                inverse_ref,
+                share_total,
+                functools.partial(wait_average, leads),
+                out,
+            )
+
+        pl.when(hub_group)(functools.partial(invert, True))
+        pl.when(group != 0)(functools.partial(invert, False))
         for k in range(1, samples_count):
             other = lax.rem(me + k, samples_count)
             copy(
@@ -740,7 +831,7 @@
 
     for item, hub in zip(energy_copies, hubs):
         pl.when(elsewhere(*hub))(item.wait_send)
-    for p, item in enumerate(out_copies):
+    for p, item in zip(far_first, out_copies):
         pl.when(elsewhere(opening + p))(item.wait_send)
 
     @pl.when(inverts & hub_group)
@@ -791,6 +882,7 @@
             kept,
             blocks,
             pltpu.VMEM((8, pair_width), F32),
+            pltpu.VMEM((pair_width, LANES), BF16),
             square,
             square,
             blocks,

time: 17.5 us -> 17.1 us (0.977)
  the two profiles are of different devices: /device:TPU:2 before, /device:TPU:1 now
where the time goes in v4:
time: 17.1 us; the launch traced here: 16.9 us
  Pallas kernels  16.3 us (95%)
  other arithmetic  0.65 us (4%)
    pallas_call x1, Pallas kernels, paired(): pl.pallas_call(functools.partial(pair_kernel, samples_count, groups_count...  16.3 us
    convert_element_type x1, other arithmetic, paired(): return pl.pallas_call(functools.partial(pair_kernel, samples_count, group...  0.65 us

profile of v4, /device:TPU:1, one launch (start us, length us, event | category | flops | bytes accessed | tf_op | source)
XLA Modules:
  0.0 16.9 jit_solution(4113931610705627687)
XLA Ops:
  0.0 16.3 %whiten.1 = f32[16,2560]{1,0:T(8,128)S(1)} custom-call(s32[8]{0:T(128)} %size_hbm.1, s32[20,128]{1,0:T(8,128)} %bitcast.1, bf16[16,2560]{1,0:T(8,128)(2,1)} %observed_hbm.1), custom_call_target="tpu_custom_call" | custom-call | tf_op jit(solution)/shard_map/whiten/pallas_call | solution.py:865
  16.3 0.6 %convert_element_type.3 = bf16[16,2560]{1,0:T(8,128)(2,1)} convert(f32[16,2560]{1,0:T(8,128)S(1)} %whiten.1) | non-fusion elementwise | flops 40960 | bytes 245760 | tf_op jit(solution)/shard_map/convert_element_type | solution.py:907

commit v5 on v4

--- a/solution.py
+++ b/solution.py
@@ -800,10 +800,10 @@
 
         pl.when(hub_group)(functools.partial(invert, True))
         pl.when(group != 0)(functools.partial(invert, False))
-        for k in range(1, samples_count):
-            other = lax.rem(me + k, samples_count)
+        for k in range(samples_count - 1):
+            other = k + (me <= k).astype(jnp.int32)
             copy(
-                done_ref.at[other], back_ref.at[mine], back_send.at[k - 1], back_recv.at[mine], other, group
+                done_ref.at[other], back_ref.at[mine], back_send.at[k], back_recv.at[mine], other, group
             ).start()
         back_ref[mine] = done_ref[me]
 
@@ -842,10 +842,10 @@
 
     @pl.when(inverts)
     def _():
-        for k in range(1, samples_count):
-            other = lax.rem(me + k, samples_count)
+        for k in range(samples_count - 1):
+            other = k + (me <= k).astype(jnp.int32)
             copy(
-                done_ref.at[other], back_ref.at[mine], back_send.at[k - 1], back_recv.at[mine], other, group
+                done_ref.at[other], back_ref.at[mine], back_send.at[k], back_recv.at[mine], other, group
             ).wait_send()
 
 

time: 17.1 us -> 17.1 us (level)
  no operation moved by 1% of the time
where the time goes in v5:
time: 17.1 us; the launch traced here: 16.9 us
  Pallas kernels  16.2 us (95%)
  other arithmetic  0.65 us (4%)
    pallas_call x1, Pallas kernels, paired(): pl.pallas_call(functools.partial(pair_kernel, samples_count, groups_count...  16.2 us
    convert_element_type x1, other arithmetic, paired(): return pl.pallas_call(functools.partial(pair_kernel, samples_count, group...  0.65 us

profile of v5, /device:TPU:1, one launch (start us, length us, event | category | flops | bytes accessed | tf_op | source)
XLA Modules:
  0.0 16.9 jit_solution(11473764737537851983)
XLA Ops:
  0.0 16.2 %whiten.1 = f32[16,2560]{1,0:T(8,128)S(1)} custom-call(s32[8]{0:T(128)} %size_hbm.1, s32[20,128]{1,0:T(8,128)} %bitcast.1, bf16[16,2560]{1,0:T(8,128)(2,1)} %observed_hbm.1), custom_call_target="tpu_custom_call" | custom-call | tf_op jit(solution)/shard_map/whiten/pallas_call | solution.py:865
  16.2 0.6 %convert_element_type.3 = bf16[16,2560]{1,0:T(8,128)(2,1)} convert(f32[16,2560]{1,0:T(8,128)S(1)} %whiten.1) | non-fusion elementwise | flops 40960 | bytes 245760 | tf_op jit(solution)/shard_map/convert_element_type | solution.py:907

commit v6 on v5

--- a/solution.py
+++ b/solution.py
@@ -645,8 +645,8 @@
 
     @pl.when(inverts)
     def _():
-        for k in range(1, samples_count):
-            signal(lax.rem(me + k, samples_count), group)
+        for k in range(samples_count - 1):
+            signal(k + (me <= k).astype(jnp.int32), group)
 
     @pl.when(inverts & hub_group)
     def _():

time: 17.1 us -> 17.1 us (level)
  no operation moved by 1% of the time
where the time goes in v6:
time: 17.1 us; the launch traced here: 16.9 us
  Pallas kernels  16.2 us (95%)
  other arithmetic  0.65 us (4%)
    pallas_call x1, Pallas kernels, paired(): pl.pallas_call(functools.partial(pair_kernel, samples_count, groups_count...  16.2 us
    convert_element_type x1, other arithmetic, paired(): return pl.pallas_call(functools.partial(pair_kernel, samples_count, group...  0.65 us

profile of v6, /device:TPU:1, one launch (start us, length us, event | category | flops | bytes accessed | tf_op | source)
XLA Modules:
  0.0 16.9 jit_solution(14049285810985512560)
XLA Ops:
  0.0 16.2 %whiten.1 = f32[16,2560]{1,0:T(8,128)S(1)} custom-call(s32[8]{0:T(128)} %size_hbm.1, s32[20,128]{1,0:T(8,128)} %bitcast.1, bf16[16,2560]{1,0:T(8,128)(2,1)} %observed_hbm.1), custom_call_target="tpu_custom_call" | custom-call | tf_op jit(solution)/shard_map/whiten/pallas_call | solution.py:865
  16.2 0.6 %convert_element_type.3 = bf16[16,2560]{1,0:T(8,128)(2,1)} convert(f32[16,2560]{1,0:T(8,128)S(1)} %whiten.1) | non-fusion elementwise | flops 40960 | bytes 245760 | tf_op jit(solution)/shard_map/convert_element_type | solution.py:907
